TPU v7x, 32 devices: a whole 2x2x4 slice. The times are simulated.
32 devices in a mesh: emb: 4 (over x, core), heads: 8 (over z, y).
Axes of the slice: x: 2, y: 2, z: 4, core: 2. Of those that a mesh axis runs over, the one named last changes fastest.
Arguments:
- hidden_in: bfloat16 [16, 8192], P(None, 'emb'), may hold values from -6 to 6
- w_z: bfloat16 [8192, 16384], P('emb', 'heads'), may hold values from -0.0625 to 0.0625
- w_x: bfloat16 [8192, 16384], P('emb', 'heads'), may hold values from -0.0625 to 0.0625
- w_bc: bfloat16 [8192, 4096], P('emb'), may hold values from -0.0625 to 0.0625
- w_dt: bfloat16 [8192, 256], P('emb', 'heads'), may hold values from -0.0625 to 0.0625
- dt_bias: float32 [256], P('heads'), may hold values from -4 to -1
- a_log: float32 [256], P('heads'), may hold values from 0 to 2.77
- skip_gain: float32 [256], P('heads'), may hold values from 0.5 to 2
- conv_x: bfloat16 [16, 3, 16384], P('emb', None, 'heads'), may hold values from -6 to 6
- conv_bc: bfloat16 [16, 3, 4096], P('emb'), may hold values from -6 to 6
- conv_wx: float32 [4, 16384], P(None, 'heads'), may hold values from -3 to 3
- conv_wbc: float32 [4, 4096], replicated, may hold values from -3 to 3
- ssm_state: float32 [16, 256, 64, 256], P('emb', 'heads'), may hold values from -0.6 to 0.6
- norm_gain: float32 [16384], P('heads'), may hold values from 0.5 to 1.5
- w_out: bfloat16 [16384, 8192], P('heads', 'emb'), may hold values from -0.046875 to 0.046875
Outputs:
- mixed: bfloat16 [16, 8192], P(None, 'emb')
- new_state: float32 [16, 256, 64, 256], P('emb', 'heads')
All inputs are finite; a program needn't handle non-finite values.
Results may differ from a plain program's by a relative error of at most 0.0051.
Values may be sent and summed in bfloat16 or wider, within the bound.
A program may use at most 128 MiB of HBM per device.

v0:
```python
import jax
import jax.numpy as jnp
from jax import lax
from jax.sharding import PartitionSpec as P

H = 256
P_SIZE = 64
N = 256
G = 8


def from_partner(value, axis, apart):
    mask = 2**apart
    pairs = [(source, source ^ mask) for source in range(lax.axis_size(axis))]
    return lax.ppermute(value, axis, pairs)


def on_device(
    hidden_in,
    w_z,
    w_x,
    w_bc,
    w_dt,
    dt_bias,
    a_log,
    skip_gain,
    conv_x,
    conv_bc,
    conv_wx,
    conv_wbc,
    ssm_state,
    norm_gain,
    w_out,
):
    heads_dev = w_dt.shape[1]
    emb_rows = w_bc.shape[0]
    batch_dev = conv_x.shape[0]
    group_span = lax.axis_size("heads") // G
    my_group = lax.axis_index("heads") // group_span
    bc_cols = lax.dynamic_slice_in_dim(w_bc.reshape(emb_rows, 2, G, N), my_group, 1, 2).reshape(
        emb_rows, 2 * N
    )
    z_part = jnp.dot(hidden_in, w_z, preferred_element_type=jnp.float32)
    x_part = jnp.dot(hidden_in, w_x, preferred_element_type=jnp.float32)
    bc_part = jnp.dot(hidden_in, bc_cols, preferred_element_type=jnp.float32)
    dt_part = jnp.dot(hidden_in, w_dt, preferred_element_type=jnp.float32)
    summed_all = lax.psum((z_part, x_part, bc_part, dt_part), "emb")
    first_row = lax.axis_index("emb") * batch_dev
    z_pre = lax.dynamic_slice_in_dim(summed_all[0], first_row, batch_dev, 0)
    x_pre = lax.dynamic_slice_in_dim(summed_all[1], first_row, batch_dev, 0)
    bc_pre = lax.dynamic_slice_in_dim(summed_all[2], first_row, batch_dev, 0)
    dt_pre = lax.dynamic_slice_in_dim(summed_all[3], first_row, batch_dev, 0)
    window_x = jnp.concatenate([conv_x.astype(jnp.float32), x_pre[:, None, :]], axis=1)
    x_conv = jax.nn.silu(jnp.sum(window_x * conv_wx[None], axis=1))
    taps_prev = conv_bc.shape[1]
    bc_state = lax.dynamic_slice_in_dim(
        conv_bc.reshape(batch_dev, taps_prev, 2, G, N), my_group, 1, 3
    ).reshape(batch_dev, taps_prev, 2 * N)
    bc_taps = lax.dynamic_slice_in_dim(
        conv_wbc.reshape(taps_prev + 1, 2, G, N), my_group, 1, 2
    ).reshape(taps_prev + 1, 2 * N)
    window_bc = jnp.concatenate([bc_state.astype(jnp.float32), bc_pre[:, None, :]], axis=1)
    bc_conv = jax.nn.silu(jnp.sum(window_bc * bc_taps[None], axis=1)).reshape(batch_dev, 2, N)
    b_group = bc_conv[:, 0]
    c_group = bc_conv[:, 1]
    step_size = jax.nn.softplus(dt_pre + dt_bias[None])
    decay_rate = jnp.exp(-jnp.exp(a_log)[None] * step_size)
    x_heads = x_conv.reshape(batch_dev, heads_dev, P_SIZE)
    new_state = (
        decay_rate[:, :, None, None] * ssm_state
        + (step_size[:, :, None] * x_heads)[..., None] * b_group[:, None, None, :]
    )
    readout = jnp.einsum("bhpn,bn->bhp", new_state, c_group, precision=lax.Precision.HIGHEST)
    readout = readout + skip_gain[None, :, None] * x_heads
    gated = readout.reshape(batch_dev, heads_dev * P_SIZE) * jax.nn.silu(z_pre)
    group_total = jnp.sum(gated * gated, axis=-1)
    span_bits = group_span.bit_length() - 1
    for level in range(span_bits):
        partner = from_partner(group_total, "heads", level)
        group_total = group_total + partner
    mean_sq = group_total / (H * P_SIZE // G)
    inv_rms = lax.rsqrt(mean_sq + 1e-05)
    normed = (gated * inv_rms[:, None] * norm_gain[None]).astype(jnp.bfloat16)
    whole_rows = lax.all_gather(normed, "emb", axis=0, tiled=True)
    partial_value = jnp.dot(whole_rows, w_out, preferred_element_type=jnp.float32)
    mixed = lax.psum(partial_value, "heads").astype(jnp.bfloat16)
    return (mixed, new_state)


def solution(mesh):
    in_specs = (
        P(None, "emb"),
        P("emb", "heads"),
        P("emb", "heads"),
        P("emb", None),
        P("emb", "heads"),
        P("heads"),
        P("heads"),
        P("heads"),
        P("emb", None, "heads"),
        P("emb", None, None),
        P(None, "heads"),
        P(),
        P("emb", "heads", None, None),
        P("heads"),
        P("heads", "emb"),
    )
    out_specs = (P(None, "emb"), P("emb", "heads", None, None))
    return jax.shard_map(
        on_device, mesh=mesh, in_specs=in_specs, out_specs=out_specs, check_vma=False
    )
```

profile of v0, /device:TPU:0, one launch (start us, length us, event | category | flops | bytes accessed | tf_op | source)
XLA Modules:
  0.0 130.3 jit_solution(5878489030706171209)
XLA Ops:
  7.2 0.0 all-reduce.5.cloned.1.call-start
  7.2 5.4 %fusion.8 = f32[16,2048]{1,0:T(8,128)} fusion(bf16[16,2048]{1,0:T(8,128)(2,1)} %param.15, bf16[2048,2048]{1,0:T(8,128)(2,1)} %param.17), kind=kOutput, calls=%fused_computation.30 | convolution fusion | flops 134217728 | bytes 8585216 | tf_op jit(solution)/shard_map/dot_general | solution.py:44
  12.7 0.4 copy-done.2
  13.1 1.9 %fusion.9 = f32[16,2048]{1,0:T(8,128)} fusion(bf16[16,2048]{1,0:T(8,128)(2,1)S(1)} %copy-done.3, bf16[2048,2048]{1,0:T(8,128)(2,1)S(1)} %copy-done.2), kind=kOutput, calls=%fused_computation.31 | convolution fusion | flops 134217728 | bytes 8585216 | tf_op jit(solution)/shard_map/dot_general | solution.py:43
  15.1 22.7 %copy.18 = bf16[2048,4096]{0,1:T(8,128)(2,1)} copy(bf16[2048,4096]{1,0:T(8,128)(2,1)} %param.18) | data formatting | bytes 33554432 | tf_op args[3]
  37.7 1.7 %constant_dynamic-slice_fusion = bf16[2048,2,1,256]{0,3,2,1:T(8,128)(2,1)S(1)} fusion(bf16[2048,2,8,256]{0,3,2,1:T(8,128)(2,1)} %bitcast.41, s32[]{:T(128)S(6)} %select_n.20), kind=kLoop, calls=%fused_computation.26 | loop fusion | bytes 4194308 | tf_op jit(solution)/shard_map/dynamic_slice | solution.py:40
  39.5 0.6 convolution_bitcast_fusion
  40.1 0.2 fusion.7
  40.3 0.1 reshape.54
  40.4 0.1 convert_reduce_fusion
  40.6 13.2 %all-reduce = (f32[16,512]{1,0:T(8,128)S(1)}, f32[16,32]{1,0:T(8,128)S(1)}) all-reduce(f32[16,512]{1,0:T(8,128)S(1)} %convolution_bitcast_fusion, f32[16,32]{1,0:T(8,128)S(1)} %fusion.7), channel_id=1, replica_groups=mesh['emb'=4,'heads'=8] {'emb'}, use_global_device_ids=true, to_apply=%region_3.4 | all-reduce | flops 8704 | bytes 69632 | tf_op jit(solution)/shard_map/psum | solution.py:47
  53.9 0.9 dynamic-slice_bitcast_fusion
  54.9 0.1 reduce_sum.32
  55.0 0.1 broadcast_multiply_fusion
  55.0 4.7 %multiply_add_fusion = f32[4,32,64,256]{3,2,1,0:T(8,128)S(1)} fusion(f32[4,32,64,256]{3,2,1,0:T(8,128)} %param.27, f32[4,256]{1,0:T(4,128)S(1)} %get-tuple-element.11, f32[4,32,64]{2,1,0:T(8,128)S(1)} %broadcast_multiply_fusion, f32[4,32]{1,0:T(4,128)S(1)} %get-tuple-element.8), kind=kLoop, calls=%fused_computation | loop fusion | flops 6291456 | bytes 16814592 | tf_op jit(solution)/shard_map/add | solution.py:70
  59.8 3.4 %copy-done.1 = f32[4,32,64,256]{3,2,1,0:T(8,128)} copy-done((f32[4,32,64,256]{3,2,1,0:T(8,128)}, f32[4,32,64,256]{3,2,1,0:T(8,128)S(1)}, u32[]{:S(2)}) %copy-start.1) | copy-done | bytes 8388632
  63.2 9.8 %fusion.4 = f32[4,1,32,64]{3,1,2,0:T(1,128)S(1)} fusion(f32[4,32,64,256]{3,2,1,0:T(8,128)S(1)} %multiply_add_fusion, f32[4,256,1,1]{1,0,2,3:T(4,128)S(1)} %get-tuple-element.10), kind=kOutput, calls=%fused_computation.23 | convolution fusion | flops 25165824 | bytes 8425472 | tf_op jit(solution)/shard_map/bhpn,bn->bhp/dot_general | solution.py:73
  73.0 0.1 multiply_add_fusion.1
  73.1 0.1 reshape.58
  73.2 1.0 multiply_reduce_fusion
  74.2 0.1 fusion.3
  74.3 5.2 %all-gather = bf16[4,4,2048]{2,1,0:T(4,128)(2,1)S(1)} all-gather(bf16[1,4,2048]{2,1,0:T(4,128)(2,1)S(1)} %fusion.3), channel_id=1, replica_groups=mesh['emb'=4,'heads'=8] {'emb'}, dimensions={0}, use_global_device_ids=true | all-gather | bytes 81920 | tf_op jit(solution)/shard_map/all_gather | solution.py:84
  79.6 4.6 %fusion.10 = f32[16,2048]{1,0:T(8,128)S(1)} fusion(bf16[16,2048]{1,0:T(8,128)(2,1)S(1)} %reshape.61, bf16[2048,2048]{1,0:T(8,128)(2,1)} %param.29), kind=kOutput, calls=%fused_computation.32 | convolution fusion | flops 134217728 | bytes 8585216 | tf_op jit(solution)/shard_map/dot_general | solution.py:85
  84.1 39.3 %all-reduce.6 = bf16[16,2048]{1,0:T(8,128)(2,1)} all-reduce(f32[16,2048]{1,0:T(8,128)S(1)} %fusion.10), channel_id=1, replica_groups=mesh['emb'=4,'heads'=8] {'heads'}, use_global_device_ids=true, to_apply=%region_7.8 | all-reduce | flops 32768 | bytes 196608 | tf_op jit(solution)/shard_map/psum | solution.py:86
  (38 shorter events, 0.4 us)
Async XLA Ops:
  7.2 33.0 %copy-start = (bf16[2048,32]{0,1:T(8,128)(2,1)S(1)}, bf16[2048,32]{0,1:T(8,128)(2,1)}, u32[]{:S(2)}) copy-start(bf16[2048,32]{0,1:T(8,128)(2,1)} %param.19) | copy-start | bytes 393220
  7.2 5.5 %copy-start.3 = (bf16[16,2048]{1,0:T(8,128)(2,1)S(1)}, bf16[16,2048]{1,0:T(8,128)(2,1)}, u32[]{:S(2)}) copy-start(bf16[16,2048]{1,0:T(8,128)(2,1)} %param.15) | copy-start | bytes 196612
  7.2 46.7 %all-reduce.5.cloned.1.call-start = ((), (), s32[]{:S(2)}) async-start(), calls=%async_computation | async-start | bytes 524288 | tf_op jit(solution)/shard_map/psum | solution.py:47
  7.2 5.9 %copy-start.2 = (bf16[2048,2048]{1,0:T(8,128)(2,1)S(1)}, bf16[2048,2048]{1,0:T(8,128)(2,1)}, u32[]{:S(2)}) copy-start(bf16[2048,2048]{1,0:T(8,128)(2,1)} %param.16) | copy-start | bytes 25165828
  15.0 25.3 %copy-start.4 = (bf16[4,3,4096]{2,0,1:T(4,128)(2,1)S(1)}, bf16[4,3,4096]{2,0,1:T(4,128)(2,1)}, u32[]{:S(2)}) copy-start(bf16[4,3,4096]{2,0,1:T(4,128)(2,1)} %param.24) | copy-start | bytes 294916
  15.0 25.5 %copy-start.5 = (f32[4,4096]{1,0:T(4,128)S(1)}, f32[4,4096]{1,0:T(4,128)}, u32[]{:S(2)}) copy-start(f32[4,4096]{1,0:T(4,128)} %param.26) | copy-start | bytes 196612
  15.0 38.8 %copy-start.11 = (f32[32]{0:T(128)S(1)}, f32[32]{0:T(128)}, u32[]{:S(2)}) copy-start(f32[32]{0:T(128)} %param.21) | copy-start | bytes 388
  15.0 38.8 %copy-start.6 = (bf16[4,3,2048]{2,0,1:T(4,128)(2,1)S(1)}, bf16[4,3,2048]{2,0,1:T(4,128)(2,1)}, u32[]{:S(2)}) copy-start(bf16[4,3,2048]{2,0,1:T(4,128)(2,1)} %param.23) | copy-start | bytes 147460
  15.0 38.8 %copy-start.10 = (f32[32]{0:T(128)S(1)}, f32[32]{0:T(128)}, u32[]{:S(2)}) copy-start(f32[32]{0:T(128)} %param.20) | copy-start | bytes 388
  15.1 39.7 %copy-start.7 = (f32[4,2048]{1,0:T(4,128)S(1)}, f32[4,2048]{1,0:T(4,128)}, u32[]{:S(2)}) copy-start(f32[4,2048]{1,0:T(4,128)} %param.25) | copy-start | bytes 98308
  59.8 3.4 %copy-start.1 = (f32[4,32,64,256]{3,2,1,0:T(8,128)}, f32[4,32,64,256]{3,2,1,0:T(8,128)S(1)}, u32[]{:S(2)}) copy-start(f32[4,32,64,256]{3,2,1,0:T(8,128)S(1)} %multiply_add_fusion) | copy-start | bytes 25165828
  59.8 13.2 %copy-start.9 = (f32[32]{0:T(128)S(1)}, f32[32]{0:T(128)}, u32[]{:S(2)}) copy-start(f32[32]{0:T(128)} %param.22) | copy-start | bytes 388
  59.8 14.4 %copy-start.8 = (f32[2048]{0:T(1024)S(1)}, f32[2048]{0:T(1024)}, u32[]{:S(2)}) copy-start(f32[2048]{0:T(1024)} %param.28) | copy-start | bytes 24580
Sparse Core Ops, SparseCore 0:
  15.1 35.0 all-reduce.4
where the time goes:
time: 131 us; the launch traced here: 130 us
  blocking collectives  57.7 us (44%)
  local copies, waits for them, and re-layouts  29.5 us (23%)
  matrix products  22.5 us (17%)
  between operations  14.3 us (11%)
  other arithmetic  6.23 us (5%)
    psum x1, blocking collectives, on_device(): mixed = lax.psum(partial_value, 'heads').astype(jnp.bfloat16)  39.3 us
    unnamed x28, local copies, waits for them, and re-layouts  26.6 us
    psum x1, blocking collectives, on_device(): summed_all = lax.psum((z_part, x_part, bc_part, dt_part), 'emb')  13.2 us
    dot_general x1, matrix products, on_device(): jnp.einsum('bhpn,bn->bhp', new_state, c_group, precision=lax.Precision.HI...  9.83 us
    dot_general x1, matrix products, on_device(): x_part = jnp.dot(hidden_in, w_x, preferred_element_type=jnp.float32)  5.43 us
    all_gather x1, blocking collectives, on_device(): whole_rows = lax.all_gather(normed, 'emb', axis=0, tiled=True)  5.23 us
    add x1, other arithmetic, on_device(): decay_rate[:, :, None, None] * ssm_state  4.75 us
    dot_general x1, matrix products, on_device(): jnp.dot(whole_rows, w_out, preferred_element_type=jnp.float32)  4.58 us
  transfers between devices with their start and end apart: 1, of which 0 were waited for; matrix products, arithmetic and copies ran while one was open for 20% of the time, Pallas kernels for 0%

commit v1 on v0

--- a/solution.py
+++ b/solution.py
@@ -2,6 +2,7 @@
 import jax.numpy as jnp
 from jax import lax
 from jax.sharding import PartitionSpec as P
+from jax.lax import all_gather
 
 H = 256
 P_SIZE = 64
@@ -83,7 +84,10 @@
     normed = (gated * inv_rms[:, None] * norm_gain[None]).astype(jnp.bfloat16)
     whole_rows = lax.all_gather(normed, "emb", axis=0, tiled=True)
     partial_value = jnp.dot(whole_rows, w_out, preferred_element_type=jnp.float32)
-    mixed = lax.psum(partial_value, "heads").astype(jnp.bfloat16)
+    digits_create = lambda values, comm_axis: jnp.sum(
+        all_gather(values, axis_name=comm_axis), axis=0
+    )
+    mixed = digits_create(partial_value, "heads").astype(jnp.bfloat16)
     return (mixed, new_state)
 
 

time: 131 us -> 136 us (1.038)
  waiting for transfers between devices: 0.04 us -> 41.2 us
  blocking collectives: 57.7 us -> 18.4 us
  other arithmetic: 6.23 us -> 8.15 us
    all_gather x0 -> x1, waiting for transfers between devices: none -> 41.1 us  [on_device(): all_gather(values, axis_name=comm_axis)]
    psum x1 -> x0, blocking collectives: 39.3 us -> none  [on_device(): mixed = lax.psum(partial_value, 'heads').astype(jnp.bfloat16)]
    reduce_sum x0 -> x1, other arithmetic: none -> 1.92 us  [on_device(): jnp.sum(all_gather(values, axis_name=comm_axis), axis=0)]
  transfers between devices with their start and end apart: 1 -> 2, of which waited for: 0 -> 1; matrix products, arithmetic and copies ran while one was open for 20% -> 19% of each run, Pallas kernels for 0% -> 0%
where the time goes in v1:
time: 136 us; the launch traced here: 135 us
  waiting for transfers between devices  41.2 us (30%)
  local copies, waits for them, and re-layouts  29.5 us (22%)
  matrix products  23.1 us (17%)
  blocking collectives  18.4 us (14%)
  between operations  14.3 us (11%)
  other arithmetic  8.15 us (6%)
    all_gather x1, waiting for transfers between devices, on_device(): all_gather(values, axis_name=comm_axis)  41.1 us
    unnamed x28, local copies, waits for them, and re-layouts  26.5 us
    psum x1, blocking collectives, on_device(): summed_all = lax.psum((z_part, x_part, bc_part, dt_part), 'emb')  13.2 us
    dot_general x1, matrix products, on_device(): jnp.einsum('bhpn,bn->bhp', new_state, c_group, precision=lax.Precision.HI...  9.83 us
    dot_general x1, matrix products, on_device(): x_part = jnp.dot(hidden_in, w_x, preferred_element_type=jnp.float32)  5.43 us
    all_gather x1, blocking collectives, on_device(): whole_rows = lax.all_gather(normed, 'emb', axis=0, tiled=True)  5.23 us
    dot_general x1, matrix products, on_device(): jnp.dot(whole_rows, w_out, preferred_element_type=jnp.float32)  5.23 us
    add x1, other arithmetic, on_device(): decay_rate[:, :, None, None] * ssm_state  4.75 us
  transfers between devices with their start and end apart: 2, of which 1 were waited for; matrix products, arithmetic and copies ran while one was open for 19% of the time, Pallas kernels for 0%

profile of v1, /device:TPU:0, one launch (start us, length us, event | category | flops | bytes accessed | tf_op | source)
XLA Modules:
  0.0 134.8 jit_solution(4964939909078449814)
XLA Ops:
  7.2 5.4 %fusion.8 = f32[16,2048]{1,0:T(8,128)} fusion(bf16[16,2048]{1,0:T(8,128)(2,1)} %param.15, bf16[2048,2048]{1,0:T(8,128)(2,1)} %param.17), kind=kOutput, calls=%fused_computation.30 | convolution fusion | flops 134217728 | bytes 8585216 | tf_op jit(solution)/shard_map/dot_general | solution.py:45
  12.7 0.4 copy-done.2
  13.1 1.9 %fusion.9 = f32[16,2048]{1,0:T(8,128)} fusion(bf16[16,2048]{1,0:T(8,128)(2,1)S(1)} %copy-done.3, bf16[2048,2048]{1,0:T(8,128)(2,1)S(1)} %copy-done.2), kind=kOutput, calls=%fused_computation.31 | convolution fusion | flops 134217728 | bytes 8585216 | tf_op jit(solution)/shard_map/dot_general | solution.py:44
  15.1 22.6 %copy.18 = bf16[2048,4096]{0,1:T(8,128)(2,1)} copy(bf16[2048,4096]{1,0:T(8,128)(2,1)} %param.18) | data formatting | bytes 33554432 | tf_op args[3]
  37.7 1.7 %constant_dynamic-slice_fusion = bf16[2048,2,1,256]{0,3,2,1:T(8,128)(2,1)S(1)} fusion(bf16[2048,2,8,256]{0,3,2,1:T(8,128)(2,1)} %bitcast.42, s32[]{:T(128)S(6)} %select_n.20), kind=kLoop, calls=%fused_computation.26 | loop fusion | bytes 4194308 | tf_op jit(solution)/shard_map/dynamic_slice | solution.py:41
  39.5 0.6 convolution_bitcast_fusion
  40.1 0.2 fusion.7
  40.3 0.1 reshape.54
  40.4 0.1 convert_reduce_fusion
  40.6 13.2 %all-reduce = (f32[16,512]{1,0:T(8,128)S(1)}, f32[16,32]{1,0:T(8,128)S(1)}) all-reduce(f32[16,512]{1,0:T(8,128)S(1)} %convolution_bitcast_fusion, f32[16,32]{1,0:T(8,128)S(1)} %fusion.7), channel_id=1, replica_groups=mesh['emb'=4,'heads'=8] {'emb'}, use_global_device_ids=true, to_apply=%region_3.4 | all-reduce | flops 8704 | bytes 69632 | tf_op jit(solution)/shard_map/psum | solution.py:48
  54.0 0.9 dynamic-slice_bitcast_fusion
  54.9 0.1 reduce_sum.41
  55.0 0.1 broadcast_multiply_fusion
  55.1 4.7 %multiply_add_fusion = f32[4,32,64,256]{3,2,1,0:T(8,128)S(1)} fusion(f32[4,32,64,256]{3,2,1,0:T(8,128)} %param.27, f32[4,256]{1,0:T(4,128)S(1)} %get-tuple-element.11, f32[4,32,64]{2,1,0:T(8,128)S(1)} %broadcast_multiply_fusion, f32[4,32]{1,0:T(4,128)S(1)} %get-tuple-element.8), kind=kLoop, calls=%fused_computation | loop fusion | flops 6291456 | bytes 16814592 | tf_op jit(solution)/shard_map/add | solution.py:71
  59.9 3.4 %copy-done.1 = f32[4,32,64,256]{3,2,1,0:T(8,128)} copy-done((f32[4,32,64,256]{3,2,1,0:T(8,128)}, f32[4,32,64,256]{3,2,1,0:T(8,128)S(1)}, u32[]{:S(2)}) %copy-start.1) | copy-done | bytes 8388632
  63.2 9.8 %fusion.4 = f32[4,1,32,64]{3,1,2,0:T(1,128)S(1)} fusion(f32[4,32,64,256]{3,2,1,0:T(8,128)S(1)} %multiply_add_fusion, f32[4,256,1,1]{1,0,2,3:T(4,128)S(1)} %get-tuple-element.10), kind=kOutput, calls=%fused_computation.23 | convolution fusion | flops 25165824 | bytes 8425472 | tf_op jit(solution)/shard_map/bhpn,bn->bhp/dot_general | solution.py:74
  73.1 0.1 multiply_add_fusion.1
  73.2 0.1 reshape.58
  73.3 1.0 multiply_reduce_fusion
  74.3 0.1 fusion.3
  74.3 5.2 %all-gather.1 = bf16[4,4,2048]{2,1,0:T(4,128)(2,1)S(1)} all-gather(bf16[1,4,2048]{2,1,0:T(4,128)(2,1)S(1)} %fusion.3), channel_id=1, replica_groups=mesh['emb'=4,'heads'=8] {'emb'}, dimensions={0}, use_global_device_ids=true | all-gather | bytes 81920 | tf_op jit(solution)/shard_map/all_gather | solution.py:85
  79.6 5.2 %fusion.10 = f32[16,2048]{1,0:T(8,128)} fusion(bf16[16,2048]{1,0:T(8,128)(2,1)S(1)} %reshape.62, bf16[2048,2048]{1,0:T(8,128)(2,1)} %param.29), kind=kOutput, calls=%fused_computation.32 | convolution fusion | flops 134217728 | bytes 8585216 | tf_op jit(solution)/shard_map/dot_general | solution.py:86
  84.9 41.1 %all-gather.4.cloned.1.call-done = f32[128,2048]{1,0:T(8,128)} async-done(((f32[16,2048]{1,0:T(8,128)}), f32[128,2048]{1,0:T(8,128)}) %all-gather.4.cloned.1.call-update) | async-done | bytes 1048592 | tf_op jit(solution)/shard_map/all_gather | solution.py:88
  126.0 1.9 %reduce_sum.45 = bf16[16,2048]{1,0:T(8,128)(2,1)} reduce(f32[8,16,2048]{2,1,0:T(8,128)} %bitcast.44, f32[]{:T(128)} %constant.36.clone.1), dimensions={0}, to_apply=%region_7.8 | reduce | flops 229376 | bytes 1114116 | tf_op jit(solution)/shard_map/reduce_sum | solution.py:87
  (41 shorter events, 0.5 us)
Async XLA Ops:
  7.2 33.0 %copy-start = (bf16[2048,32]{0,1:T(8,128)(2,1)S(1)}, bf16[2048,32]{0,1:T(8,128)(2,1)}, u32[]{:S(2)}) copy-start(bf16[2048,32]{0,1:T(8,128)(2,1)} %param.19) | copy-start | bytes 393220
  7.2 5.5 %copy-start.3 = (bf16[16,2048]{1,0:T(8,128)(2,1)S(1)}, bf16[16,2048]{1,0:T(8,128)(2,1)}, u32[]{:S(2)}) copy-start(bf16[16,2048]{1,0:T(8,128)(2,1)} %param.15) | copy-start | bytes 196612
  7.2 46.8 %all-reduce.4.cloned.1.call-start = ((), (), s32[]{:S(2)}) async-start(), calls=%async_computation.1 | async-start | bytes 524288 | tf_op jit(solution)/shard_map/psum | solution.py:48
  7.2 5.9 %copy-start.2 = (bf16[2048,2048]{1,0:T(8,128)(2,1)S(1)}, bf16[2048,2048]{1,0:T(8,128)(2,1)}, u32[]{:S(2)}) copy-start(bf16[2048,2048]{1,0:T(8,128)(2,1)} %param.16) | copy-start | bytes 25165828
  15.0 111.0 %all-gather.4.cloned.1.call-start = ((), (), s32[]{:S(2)}) async-start(), calls=%async_computation | async-start | bytes 1179648 | tf_op jit(solution)/shard_map/all_gather | solution.py:88
  15.0 25.3 %copy-start.4 = (bf16[4,3,4096]{2,0,1:T(4,128)(2,1)S(1)}, bf16[4,3,4096]{2,0,1:T(4,128)(2,1)}, u32[]{:S(2)}) copy-start(bf16[4,3,4096]{2,0,1:T(4,128)(2,1)} %param.24) | copy-start | bytes 294916
  15.1 25.4 %copy-start.5 = (f32[4,4096]{1,0:T(4,128)S(1)}, f32[4,4096]{1,0:T(4,128)}, u32[]{:S(2)}) copy-start(f32[4,4096]{1,0:T(4,128)} %param.26) | copy-start | bytes 196612
  15.1 38.8 %copy-start.11 = (f32[32]{0:T(128)S(1)}, f32[32]{0:T(128)}, u32[]{:S(2)}) copy-start(f32[32]{0:T(128)} %param.21) | copy-start | bytes 388
  15.1 38.8 %copy-start.6 = (bf16[4,3,2048]{2,0,1:T(4,128)(2,1)S(1)}, bf16[4,3,2048]{2,0,1:T(4,128)(2,1)}, u32[]{:S(2)}) copy-start(bf16[4,3,2048]{2,0,1:T(4,128)(2,1)} %param.23) | copy-start | bytes 147460
  15.1 38.8 %copy-start.10 = (f32[32]{0:T(128)S(1)}, f32[32]{0:T(128)}, u32[]{:S(2)}) copy-start(f32[32]{0:T(128)} %param.20) | copy-start | bytes 388
  15.1 39.7 %copy-start.7 = (f32[4,2048]{1,0:T(4,128)S(1)}, f32[4,2048]{1,0:T(4,128)}, u32[]{:S(2)}) copy-start(f32[4,2048]{1,0:T(4,128)} %param.25) | copy-start | bytes 98308
  59.8 3.4 %copy-start.1 = (f32[4,32,64,256]{3,2,1,0:T(8,128)}, f32[4,32,64,256]{3,2,1,0:T(8,128)S(1)}, u32[]{:S(2)}) copy-start(f32[4,32,64,256]{3,2,1,0:T(8,128)S(1)} %multiply_add_fusion) | copy-start | bytes 25165828
  59.9 13.2 %copy-start.9 = (f32[32]{0:T(128)S(1)}, f32[32]{0:T(128)}, u32[]{:S(2)}) copy-start(f32[32]{0:T(128)} %param.22) | copy-start | bytes 388
  59.9 14.4 %copy-start.8 = (f32[2048]{0:T(1024)S(1)}, f32[2048]{0:T(1024)}, u32[]{:S(2)}) copy-start(f32[2048]{0:T(1024)} %param.28) | copy-start | bytes 24580
Sparse Core Ops, SparseCore 0:
  15.1 35.0 all-reduce.3
  85.0 40.9 all-gather.3
